TPU v7x, 32 devices: a whole 2x2x4 slice. The times are simulated.
32 devices in a mesh: dp: 8 (over z, y), fsdp: 4 (over x, core).
Axes of the slice: x: 2, y: 2, z: 4, core: 2. Of those that a mesh axis runs over, the one named last changes fastest.
Arguments:
- tokens: bfloat16 [16384, 4096], P(('dp', 'fsdp')), may hold values from -0.75 to 0.75
- doc_ids: int32 [16384], P(('dp', 'fsdp')), may hold values from 0 to 15, never falling along the last dimension, each value on 1 to 2048 neighbouring positions
- attn_gain: float32 [4096], replicated, may hold values from 0.1 to 1.9
- mlp_gain: float32 [4096], replicated, may hold values from 0.1 to 1.9
- w_query: bfloat16 [4096, 512], P(('dp', 'fsdp')), may hold values from -1 to 1
- w_key_value: bfloat16 [4096, 256], P(('dp', 'fsdp')), may hold values from -3 to 3
- w_out: bfloat16 [512, 4096], P(None, ('dp', 'fsdp')), may hold values from -0.25 to 0.25
- w_gate: bfloat16 [4096, 1024], P(('dp', 'fsdp')), may hold values from -0.09375 to 0.09375
- w_up: bfloat16 [4096, 1024], P(('dp', 'fsdp')), may hold values from -0.09375 to 0.09375
- w_down: bfloat16 [1024, 4096], P(None, ('dp', 'fsdp')), may hold values from -0.1875 to 0.1875
Outputs:
- mixed: bfloat16 [16384, 4096], P(('dp', 'fsdp'))
Inputs may be any that keep to these rules, and one draw needn't show every extreme that they name: `doc_ids`: document numbers never fall along the pack, and every document has at most 2048 tokens.
All inputs are finite; a program needn't handle non-finite values.
Results may differ from a plain program's by a relative error of at most 0.02.
The roundings to bfloat16 on the way count: a program that leaves them out, or rounds other values in their place, can miss the bound.
Values may be sent and summed in bfloat16 or wider, within the bound.
A program may use at most 128 MiB of HBM per device.

v0:
```python
import math
import jax
import jax.numpy as jnp
from jax import lax
from jax.sharding import PartitionSpec as P

SPAN = 4
EPS = 1e-05
THETA = 500000.0
NEGATIVE = -1e30


def shifted(array, axis, by):
    length = lax.axis_size(axis)
    pairs = [(i, i + by) for i in range(length) if 0 <= i + by < length]
    return lax.ppermute(array, axis, pairs)


def rms_scale(values, gain):
    wide = values.astype(jnp.float32)
    power = jnp.mean(wide * wide, axis=-1, keepdims=True)
    return (wide * lax.rsqrt(power + EPS) * gain).astype(jnp.bfloat16)


def rotate(values, position):
    head = values.shape[-1]
    half = head // 2
    freqs = THETA ** (-2.0 * jnp.arange(half, dtype=jnp.float32) / head)
    angle = position.astype(jnp.float32)[:, None, None] * freqs[None, None, :]
    cosine = jnp.cos(angle)
    sine = jnp.sin(angle)
    first = values[..., :half]
    second = values[..., half:]
    return jnp.concatenate(
        [first * cosine - second * sine, second * cosine + first * sine], axis=-1
    )


def head_scores(query, keys):
    return jnp.einsum("qhd,kd->hqk", query, keys, preferred_element_type=jnp.float32) / math.sqrt(
        query.shape[-1]
    )


def weigh_values(weights, values):
    return jnp.einsum(
        "hqk,kd->qhd", weights.astype(jnp.bfloat16), values, preferred_element_type=jnp.float32
    )


def attend_dense(query, keys, values, key_marks, marks, offset):
    scores = head_scores(query, keys)
    key_index = jnp.arange(keys.shape[0], dtype=jnp.int32)
    query_index = jnp.arange(query.shape[0], dtype=jnp.int32) + offset
    allowed = (key_marks[None, :] == marks[:, None]) & (key_index[None, :] <= query_index[:, None])
    scores = jnp.where(allowed[None, :, :], scores, NEGATIVE)
    peak = jnp.max(scores, axis=2, keepdims=True)
    weights = jnp.exp(scores - peak)
    totals = jnp.sum(weights, axis=2)
    return weigh_values(weights, values) / jnp.transpose(totals)[:, :, None]


def per_device(
    tokens, doc_ids, attn_gain, mlp_gain, w_query, w_key_value, w_out, w_gate, w_up, w_down
):
    rows = tokens.shape[0]
    rank = lax.axis_index(("dp", "fsdp"))
    normed = rms_scale(tokens, attn_gain)
    query_width = w_query.shape[1]
    pair_width = w_key_value.shape[1]
    head = pair_width // 2
    heads = query_width // head
    group_query, group_pair = (
        lax.all_gather(w_query, "fsdp", axis=0, tiled=True),
        lax.all_gather(w_key_value, "fsdp", axis=0, tiled=True),
    )
    pieces = (
        lax.all_gather(group_query, "dp", axis=0, tiled=True),
        lax.all_gather(group_pair, "dp", axis=0, tiled=True),
    )
    columns = normed
    query_raw = jnp.dot(columns, pieces[0], preferred_element_type=jnp.float32)
    pair_raw = jnp.dot(columns, pieces[1], preferred_element_type=jnp.float32)
    position = rank * rows + jnp.arange(rows, dtype=jnp.int32)
    query = rotate(query_raw.reshape(rows, heads, head), position).astype(jnp.bfloat16)
    keys = rotate(pair_raw[:, None, :head], position)[:, 0, :].astype(jnp.bfloat16)
    values = pair_raw[:, head:].astype(jnp.bfloat16)
    own_pairs = jnp.concatenate([keys, values], axis=1)
    marks = doc_ids + 1
    amounts = [1] + [1 << level for level in range(SPAN.bit_length() - 1)]
    held_pairs = own_pairs
    held_marks = marks
    for order, amount in enumerate(amounts):
        moved_pairs, moved_marks = shifted((held_pairs, held_marks), ("dp", "fsdp"), amount)
        if order == 0:
            held_pairs = moved_pairs
            held_marks = moved_marks
        else:
            held_pairs = jnp.concatenate([moved_pairs, held_pairs], axis=0)
            held_marks = jnp.concatenate([moved_marks, held_marks], axis=0)
    every_pair = jnp.concatenate([held_pairs, own_pairs], axis=0)
    every_mark = jnp.concatenate([held_marks, marks], axis=0)
    mixed = attend_dense(
        query, every_pair[:, :head], every_pair[:, head:], every_mark, marks, held_pairs.shape[0]
    )
    attended = mixed.reshape(rows, query_width).astype(jnp.bfloat16)
    projected = jnp.dot(
        attended,
        lax.all_gather(w_out, ("dp", "fsdp"), axis=1, tiled=True),
        preferred_element_type=jnp.float32,
    )
    resid = (tokens.astype(jnp.float32) + projected).astype(jnp.bfloat16)
    resid = lax.optimization_barrier(resid)
    normed_mlp = rms_scale(resid, mlp_gain)
    pieces = (
        lax.all_gather(w_gate, ("dp", "fsdp"), axis=0, tiled=True),
        lax.all_gather(w_up, ("dp", "fsdp"), axis=0, tiled=True),
    )
    columns = normed_mlp
    gate = jnp.dot(columns, pieces[0], preferred_element_type=jnp.float32)
    up_value = jnp.dot(columns, pieces[1], preferred_element_type=jnp.float32)
    hidden = (jax.nn.silu(gate) * up_value).astype(jnp.bfloat16)
    down = jnp.dot(
        hidden,
        lax.all_gather(w_down, ("dp", "fsdp"), axis=1, tiled=True),
        preferred_element_type=jnp.float32,
    )
    return (resid.astype(jnp.float32) + down).astype(jnp.bfloat16)


def solution(mesh):
    in_specs = (
        P(("dp", "fsdp"), None),
        P(("dp", "fsdp")),
        P(),
        P(),
        P(("dp", "fsdp"), None),
        P(("dp", "fsdp"), None),
        P(None, ("dp", "fsdp")),
        P(("dp", "fsdp"), None),
        P(("dp", "fsdp"), None),
        P(None, ("dp", "fsdp")),
    )
    out_specs = P(("dp", "fsdp"), None)
    return jax.shard_map(
        per_device, mesh=mesh, in_specs=in_specs, out_specs=out_specs, check_vma=False
    )
```

profile of v0, /device:TPU:0, one launch (start us, length us, event | category | flops | bytes accessed | tf_op | source)
XLA Modules:
  0.0 483.1 jit_solution(8188637932389461897)
XLA Ops:
  6.5 9.0 %all_gather.24 = bf16[512,256]{1,0:T(8,128)(2,1)} all-gather(bf16[128,256]{1,0:T(8,128)(2,1)} %param.15), channel_id=1, replica_groups=mesh['dp'=8,'fsdp'=4] {'fsdp'}, dimensions={0}, use_global_device_ids=true | all-gather | bytes 327680 | tf_op jit(solution)/shard_map/all_gather | solution.py:75
  15.5 0.0 all-gather.7.cloned.1.call-update
  15.5 0.0 all-gather.9.cloned.1.call-start
  15.6 8.3 %all_gather.26 = bf16[512,512]{1,0:T(8,128)(2,1)} all-gather(bf16[128,512]{1,0:T(8,128)(2,1)} %param.14), channel_id=1, replica_groups=mesh['dp'=8,'fsdp'=4] {'fsdp'}, dimensions={0}, use_global_device_ids=true | all-gather | bytes 655360 | tf_op jit(solution)/shard_map/all_gather | solution.py:74
  23.9 0.0 all-gather.11.cloned.1.call-start
  24.0 0.7 all-gather.11.cloned.1.call-update
  24.6 0.0 all-gather.13.cloned.1.call-start
  24.7 0.5 all-gather.13.cloned.1.call-update
  25.2 0.0 all-gather.15.cloned.1.call-start
  25.3 0.5 all-gather.15.cloned.1.call-update
  25.8 0.0 all-gather.17.cloned.1.call-start
  25.9 0.5 all-gather.17.cloned.1.call-update
  26.4 3.1 fusion.6
  29.5 35.6 %all-gather.7.cloned.1.call-done = bf16[4096,256]{1,0:T(8,128)(2,1)} async-done(((bf16[512,256]{1,0:T(8,128)(2,1)}), bf16[4096,256]{1,0:T(8,128)(2,1)}) %all-gather.7.cloned.1.call-update) | async-done | bytes 2097168 | tf_op jit(solution)/shard_map/all_gather | solution.py:79
  65.1 4.4 fusion.23
  69.6 0.6 fusion.36
  70.2 1.3 collective-permute-start
  71.5 4.1 collective-permute-start.3
  75.6 0.8 collective-permute-done.3
  76.4 2.5 collective-permute-start.4
  78.9 1.0 multiply_cosine_fusion
  79.9 4.4 collective-permute-start.1
  84.4 3.4 collective-permute-start.5
  87.8 1.3 collective-permute-done.5
  89.1 0.1 pad_maximum_fusion
  89.2 4.4 collective-permute-start.2
  93.6 1.4 fusion.14
  95.0 10.2 %collective-permute-done.2 = bf16[1024,256]{0,1:T(8,128)(2,1)S(1)} collective-permute-done((bf16[1024,256]{0,1:T(8,128)(2,1)S(1)}, bf16[1024,256]{0,1:T(8,128)(2,1)S(1)}, u32[]{:S(2)}, u32[]{:S(2)}) %collective-permute-start.2) | collective-permute-done | bytes 524320 | tf_op jit(solution)/shard_map/ppermute | solution.py:16
  105.2 1.1 maximum_maximum_fusion
  106.4 44.8 %all-gather.9.cloned.1.call-done = bf16[4096,512]{1,0:T(8,128)(2,1)} async-done(((bf16[512,512]{1,0:T(8,128)(2,1)}), bf16[4096,512]{1,0:T(8,128)(2,1)}) %all-gather.9.cloned.1.call-update) | async-done | bytes 4194320 | tf_op jit(solution)/shard_map/all_gather | solution.py:78
  151.2 5.9 %fusion.21 = f32[512,512]{0,1:T(8,128)S(1)} fusion(bf16[4096,512]{1,0:T(8,128)(2,1)} %all-gather.9.cloned.1.call-done, bf16[512,4096]{1,0:T(8,128)(2,1)} %param.10, f32[4096]{0:T(1024)S(1)} %copy-done.3, f32[512]{0:T(512)S(1)} %add_rsqrt_fusion.1), kind=kOutput, calls=%fused_computation.27 | convolution fusion | flops 2155872256 | bytes 9455616 | tf_op jit(solution)/shard_map/dot_general | solution.py:82
  157.1 0.9 fusion.42
  158.1 1.4 copy.18
  159.4 1.4 copy.19
  160.8 1.5 subtract_convert_fusion
  162.4 5.3 %fusion.2 = (f32[4,512]{1,0:T(4,128)S(1)}, f32[2560,512,4]{1,0,2:T(8,128)S(1)}) fusion(pred[512,2560]{0,1:T(8,128)(4,1)S(1)} %fusion.14, bf16[512,4,64]{2,0,1:T(8,128)(2,1)S(1)} %get-tuple-element.6, bf16[512,4,64]{2,0,1:T(8,128)(2,1)S(1)} %get-tuple-element.5, bf16[2560,256]{0,1:T(8,128)(2,1)} %maximum_maximum_fusion), kind=kOutput, calls=%fused_computation.4 | convolution fusion | flops 1358952448 | bytes 23470080 | tf_op jit(solution)/shard_map/qhd,kd->hqk/dot_general | solution.py:40
  167.6 4.5 fusion
  172.2 6.1 %divide_convert_fusion = bf16[512,4,128]{0,2,1:T(8,128)(2,1)S(1)} fusion(f32[2560,512,4]{1,0,2:T(8,128)S(1)} %get-tuple-element.14, f32[4,512]{1,0:T(4,128)S(1)} %get-tuple-element.13, pred[512,2560]{0,1:T(8,128)(4,1)S(1)} %fusion.14, bf16[2560,256]{0,1:T(8,128)(2,1)S(1)} %copy-done.1, f32[512,4]{0,1:T(4,128)S(1)} %bitcast.42), kind=kOutput, calls=%fused_computation.29 | convolution fusion | flops 1363673088 | bytes 23478272 | tf_op jit(solution)/shard_map/hqk,kd->qhd/dot_general | solution.py:46
  178.3 38.3 %all-gather.11.cloned.1.call-done = bf16[512,4096]{1,0:T(8,128)(2,1)} async-done(((bf16[512,128]{1,0:T(8,128)(2,1)}), bf16[512,4096]{1,0:T(8,128)(2,1)}) %all-gather.11.cloned.1.call-update) | async-done | bytes 4194320 | tf_op jit(solution)/shard_map/all_gather | solution.py:109
  216.7 5.9 %fusion.9 = bf16[512,4096]{1,0:T(8,128)(2,1)S(1)} fusion(bf16[512,4096]{1,0:T(8,128)(2,1)} %param.10, bf16[512,512]{0,1:T(8,128)(2,1)S(1)} %bitcast.41, bf16[512,4096]{1,0:T(8,128)(2,1)} %all-gather.11.cloned.1.call-done), kind=kOutput, calls=%fused_computation.16 | convolution fusion | flops 2153775104 | bytes 13107200 | tf_op jit(solution)/shard_map/dot_general | solution.py:107
  222.6 2.0 copy-done
  224.6 0.9 fusion.10
  225.5 69.2 %all-gather.13.cloned.1.call-done = bf16[4096,1024]{1,0:T(8,128)(2,1)} async-done(((bf16[128,1024]{1,0:T(8,128)(2,1)}), bf16[4096,1024]{1,0:T(8,128)(2,1)}) %all-gather.13.cloned.1.call-update) | async-done | bytes 8388624 | tf_op jit(solution)/shard_map/all_gather | solution.py:116
  294.6 8.2 %fusion.19 = f32[512,1024]{1,0:T(8,128)S(1)} fusion(bf16[4096,1024]{1,0:T(8,128)(2,1)} %all-gather.13.cloned.1.call-done, bf16[512,4096]{1,0:T(8,128)(2,1)} %copy-done, f32[4096]{0:T(1024)S(1)} %copy-done.4, f32[512]{0:T(512)S(1)} %add_rsqrt_fusion), kind=kOutput, calls=%fused_computation.26 | convolution fusion | flops 4303355904 | bytes 14698496 | tf_op jit(solution)/shard_map/dot_general | solution.py:120
  302.9 70.2 %all-gather.15.cloned.1.call-done = bf16[4096,1024]{1,0:T(8,128)(2,1)} async-done(((bf16[128,1024]{1,0:T(8,128)(2,1)}), bf16[4096,1024]{1,0:T(8,128)(2,1)}) %all-gather.15.cloned.1.call-update) | async-done | bytes 8388624 | tf_op jit(solution)/shard_map/all_gather | solution.py:117
  373.0 9.4 %multiply_convert_fusion = bf16[512,1024]{1,0:T(8,128)(2,1)S(1)} fusion(f32[512,1024]{1,0:T(8,128)S(1)} %fusion.19, bf16[4096,1024]{1,0:T(8,128)(2,1)} %all-gather.15.cloned.1.call-done, bf16[512,4096]{1,0:T(8,128)(2,1)} %copy-done, f32[4096]{0:T(1024)S(1)} %copy-done.4, f32[512]{0:T(512)S(1)} %add_rsqrt_fusion), kind=kOutput, calls=%fused_computation.23 | convolution fusion | flops 4306501632 | bytes 15747072 | tf_op jit(solution)/shard_map/dot_general | solution.py:121
  382.4 83.8 %all-gather.17.cloned.1.call-done = bf16[1024,4096]{1,0:T(8,128)(2,1)} async-done(((bf16[1024,128]{1,0:T(8,128)(2,1)}), bf16[1024,4096]{1,0:T(8,128)(2,1)}) %all-gather.17.cloned.1.call-update) | async-done | bytes 8388624 | tf_op jit(solution)/shard_map/all_gather | solution.py:125
  466.2 10.1 %fusion.13 = bf16[512,4096]{1,0:T(8,128)(2,1)} fusion(bf16[512,4096]{1,0:T(8,128)(2,1)} %copy-done, bf16[512,1024]{1,0:T(8,128)(2,1)S(1)} %multiply_convert_fusion, bf16[1024,4096]{1,0:T(8,128)(2,1)} %all-gather.17.cloned.1.call-done), kind=kOutput, calls=%fused_computation.20 | convolution fusion | flops 4301258752 | bytes 17825792 | tf_op jit(solution)/shard_map/dot_general | solution.py:123
  (26 shorter events, 0.2 us)
Async XLA Ops:
  6.5 58.6 %copy-start.3 = (f32[4096]{0:T(1024)S(1)}, f32[4096]{0:T(1024)}, u32[]{:S(2)}) copy-start(f32[4096]{0:T(1024)} %param.12) | copy-start | bytes 49156
  6.5 58.5 %all-gather.7.cloned.1.call-start = ((), (), s32[]{:S(2)}) async-start(), calls=%async_computation | async-start | bytes 2359296 | tf_op jit(solution)/shard_map/all_gather | solution.py:79
  15.5 135.7 %all-gather.9.cloned.1.call-start = ((), (), s32[]{:S(2)}) async-start(), calls=%async_computation.1 | async-start | bytes 4718592 | tf_op jit(solution)/shard_map/all_gather | solution.py:78
  23.9 192.8 %all-gather.11.cloned.1.call-start = ((), (), s32[]{:S(2)}) async-start(), calls=%async_computation.2 | async-start | bytes 4325376 | tf_op jit(solution)/shard_map/all_gather | solution.py:109
  24.6 270.0 %all-gather.13.cloned.1.call-start = ((), (), s32[]{:S(2)}) async-start(), calls=%async_computation.3 | async-start | bytes 8650752 | tf_op jit(solution)/shard_map/all_gather | solution.py:116
  25.2 347.8 %all-gather.15.cloned.1.call-start = ((), (), s32[]{:S(2)}) async-start(), calls=%async_computation.4 | async-start | bytes 8650752 | tf_op jit(solution)/shard_map/all_gather | solution.py:117
  25.8 440.4 %all-gather.17.cloned.1.call-start = ((), (), s32[]{:S(2)}) async-start(), calls=%async_computation.5 | async-start | bytes 8650752 | tf_op jit(solution)/shard_map/all_gather | solution.py:125
  29.5 42.0 %copy-start.2 = (s32[512]{0:T(512)S(1)}, s32[512]{0:T(512)}, u32[]{:S(2)}) copy-start(s32[512]{0:T(512)} %param.11) | copy-start | bytes 6148
  70.2 9.7 %collective-permute-start = (bf16[512,256]{0,1:T(8,128)(2,1)S(1)}, bf16[512,256]{0,1:T(8,128)(2,1)S(1)}, u32[]{:S(2)}, u32[]{:S(2)}) collective-permute-start(bf16[512,256]{0,1:T(8,128)(2,1)S(1)} %pad_maximum_fusion.1), channel_id=1, source_target_pairs={{0,1},{1,2},{2,3},{3,4},{4,5},{5,6},{6,7},{7,8},{8,9},{9,10},{10,1... | collective-permute-start | bytes 786440 | tf_op jit(solution)/shard_map/ppermute | solution.py:16
  71.5 4.9 %collective-permute-start.3 = (s32[512]{0:T(512)S(1)}, s32[512]{0:T(512)S(1)}, u32[]{:S(2)}, u32[]{:S(2)}) collective-permute-start(s32[512]{0:T(512)S(1)} %broadcast_add_fusion), channel_id=1, source_target_pairs={{0,1},{1,2},{2,3},{3,4},{4,5},{5,6},{6,7},{7,8},{8,9},{9,10},{10,1... | collective-permute-start | bytes 6152 | tf_op jit(solution)/shard_map/ppermute | solution.py:16
  76.4 7.9 %collective-permute-start.4 = (s32[512]{0:T(512)S(1)}, s32[512]{0:T(512)S(1)}, u32[]{:S(2)}, u32[]{:S(2)}) collective-permute-start(s32[512]{0:T(512)S(1)} %collective-permute-done.3), channel_id=1, source_target_pairs={{0,1},{1,2},{2,3},{3,4},{4,5},{5,6},{6,7},{7,8},{8,9},{9,10},{10,1... | collective-permute-start | bytes 6152 | tf_op jit(solution)/shard_map/ppermute | solution.py:16
  79.9 9.2 %collective-permute-start.1 = (bf16[512,256]{0,1:T(8,128)(2,1)S(1)}, bf16[512,256]{0,1:T(8,128)(2,1)S(1)}, u32[]{:S(2)}, u32[]{:S(2)}) collective-permute-start(bf16[512,256]{0,1:T(8,128)(2,1)S(1)} %collective-permute-done), channel_id=1, source_target_pairs={{0,1},{1,2},{2,3},{3,4},{4,5},{5,6},{6,7},{7,8},{8,9},{9,10},{10,1... | collective-permute-start | bytes 786440 | tf_op jit(solution)/shard_map/ppermute | solution.py:16
  84.4 4.8 collective-permute-start.5
  89.2 16.1 %collective-permute-start.2 = (bf16[1024,256]{0,1:T(8,128)(2,1)S(1)}, bf16[1024,256]{0,1:T(8,128)(2,1)S(1)}, u32[]{:S(2)}, u32[]{:S(2)}) collective-permute-start(bf16[1024,256]{0,1:T(8,128)(2,1)S(1)} %pad_maximum_fusion), channel_id=1, source_target_pairs={{0,2},{1,3},{2,4},{3,5},{4,6},{5,7},{6,8},{7,9},{8,10},{9,11},{10,... | collective-permute-start | bytes 1572872 | tf_op jit(solution)/shard_map/ppermute | solution.py:16
  167.6 4.6 copy-start.1
  222.6 2.0 copy-start
  224.6 70.1 %copy-start.4 = (f32[4096]{0:T(1024)S(1)}, f32[4096]{0:T(1024)}, u32[]{:S(2)}) copy-start(f32[4096]{0:T(1024)} %param.13) | copy-start | bytes 49156
Sparse Core Ops, SparseCore 0:
  15.6 49.3 all-gather.6
  67.2 83.9 all-gather.8
  154.0 62.5 all-gather.10
  219.4 75.2 all-gather.12
  297.3 75.6 all-gather.14
  375.8 90.4 all-gather.16
where the time goes:
time: 484 us; the launch traced here: 483 us
  waiting for transfers between devices  356 us (74%)
  matrix products  55.3 us (11%)
  starting transfers between devices  20.3 us (4%)
  blocking collectives  17.3 us (4%)
  other arithmetic  14.3 us (3%)
  between operations  13.7 us (3%)
  local copies, waits for them, and re-layouts  5.75 us (1%)
    all_gather x1, waiting for transfers between devices, per_device(): lax.all_gather(w_down, ('dp', 'fsdp'), axis=1, tiled=True)  83.8 us
    all_gather x1, waiting for transfers between devices, per_device(): lax.all_gather(w_up, ('dp', 'fsdp'), axis=0, tiled=True)  70.2 us
    all_gather x1, waiting for transfers between devices, per_device(): lax.all_gather(w_gate, ('dp', 'fsdp'), axis=0, tiled=True)  69.2 us
    all_gather x1, waiting for transfers between devices, per_device(): lax.all_gather(group_query, 'dp', axis=0, tiled=True)  44.8 us
    all_gather x1, waiting for transfers between devices, per_device(): lax.all_gather(w_out, ('dp', 'fsdp'), axis=1, tiled=True)  38.3 us
    all_gather x1, waiting for transfers between devices, per_device(): lax.all_gather(group_pair, 'dp', axis=0, tiled=True)  35.6 us
    ppermute x6, starting transfers between devices, shifted(): return lax.ppermute(array, axis, pairs)  20.1 us
    ppermute x6, waiting for transfers between devices, shifted(): return lax.ppermute(array, axis, pairs)  12.3 us
  transfers between devices with their start and end apart: 12, of which 9 were waited for; matrix products, arithmetic and copies ran while one was open for 13% of the time, Pallas kernels for 0%

commit v1 on v0

--- a/solution.py
+++ b/solution.py
@@ -122,7 +122,7 @@
     hidden = (jax.nn.silu(gate) * up_value).astype(jnp.bfloat16)
     down = jnp.dot(
         hidden,
-        lax.all_gather(w_down, ("dp", "fsdp"), axis=1, tiled=True),
+        jnp.concatenate(lax.all_gather(w_down, ("dp", "fsdp")), axis=1),
         preferred_element_type=jnp.float32,
     )
     return (resid.astype(jnp.float32) + down).astype(jnp.bfloat16)

time: 484 us -> 477 us (0.986)
  waiting for transfers between devices: 356 us -> 337 us
  local copies, waits for them, and re-layouts: 5.75 us -> 17.1 us
    all_gather x1, waiting for transfers between devices: 83.8 us -> 69.2 us  [per_device(): lax.all_gather(w_down, ('dp', 'fsdp'))]
    reshape x0 -> x1, local copies, waits for them, and re-layouts: none -> 11.3 us  [per_device(): jnp.concatenate(lax.all_gather(w_down, ('dp', 'fsdp')), axis=1)]
  transfers between devices with their start and end apart: 12 -> 12, of which waited for: 9 -> 9; matrix products, arithmetic and copies ran while one was open for 13% -> 14% of each run, Pallas kernels for 0% -> 0%
where the time goes in v1:
time: 477 us
  waiting for transfers between devices  337 us (71%)
  matrix products  56.5 us (12%)
  starting transfers between devices  20.3 us (4%)
  blocking collectives  17.3 us (4%)
  local copies, waits for them, and re-layouts  17.1 us (4%)
  other arithmetic  14.3 us (3%)
  between operations  13.7 us (3%)
    all_gather x1, waiting for transfers between devices, per_device(): lax.all_gather(w_down, ('dp', 'fsdp'))  69.2 us
    all_gather x1, waiting for transfers between devices, per_device(): lax.all_gather(w_up, ('dp', 'fsdp'), axis=0, tiled=True)  67.9 us
    all_gather x1, waiting for transfers between devices, per_device(): lax.all_gather(w_gate, ('dp', 'fsdp'), axis=0, tiled=True)  67.1 us
    all_gather x1, waiting for transfers between devices, per_device(): lax.all_gather(group_query, 'dp', axis=0, tiled=True)  44.8 us
    all_gather x1, waiting for transfers between devices, per_device(): lax.all_gather(w_out, ('dp', 'fsdp'), axis=1, tiled=True)  38.3 us
    all_gather x1, waiting for transfers between devices, per_device(): lax.all_gather(group_pair, 'dp', axis=0, tiled=True)  35.6 us
    ppermute x6, starting transfers between devices, shifted(): return lax.ppermute(array, axis, pairs)  20.1 us
    ppermute x6, waiting for transfers between devices, shifted(): return lax.ppermute(array, axis, pairs)  12.3 us
  transfers between devices with their start and end apart: 12, of which 9 were waited for; matrix products, arithmetic and copies ran while one was open for 14% of the time, Pallas kernels for 0%

profile of v1, /device:TPU:0, one launch (start us, length us, event | category | flops | bytes accessed | tf_op | source)
XLA Modules:
  0.0 476.6 jit_solution(5528601957117688253)
XLA Ops:
  6.5 9.0 %all_gather.27 = bf16[512,256]{1,0:T(8,128)(2,1)} all-gather(bf16[128,256]{1,0:T(8,128)(2,1)} %param.15), channel_id=1, replica_groups=mesh['dp'=8,'fsdp'=4] {'fsdp'}, dimensions={0}, use_global_device_ids=true | all-gather | bytes 327680 | tf_op jit(solution)/shard_map/all_gather | solution.py:75
  15.5 0.0 all-gather.10.cloned.1.call-start
  15.6 8.3 %all_gather.29 = bf16[512,512]{1,0:T(8,128)(2,1)} all-gather(bf16[128,512]{1,0:T(8,128)(2,1)} %param.14), channel_id=1, replica_groups=mesh['dp'=8,'fsdp'=4] {'fsdp'}, dimensions={0}, use_global_device_ids=true | all-gather | bytes 655360 | tf_op jit(solution)/shard_map/all_gather | solution.py:74
  23.9 0.0 all-gather.12.cloned.1.call-start
  23.9 0.7 all-gather.12.cloned.1.call-update
  24.6 0.0 all-gather.18.cloned.1.call-start
  24.7 0.5 all-gather.18.cloned.1.call-update
  25.2 0.0 all-gather.14.cloned.1.call-start
  25.3 0.5 all-gather.14.cloned.1.call-update
  25.8 0.0 all-gather.16.cloned.1.call-start
  25.8 0.5 all-gather.16.cloned.1.call-update
  26.4 3.1 fusion.6
  29.5 35.6 %all-gather.8.cloned.1.call-done = bf16[4096,256]{1,0:T(8,128)(2,1)} async-done(((bf16[512,256]{1,0:T(8,128)(2,1)}), bf16[4096,256]{1,0:T(8,128)(2,1)}) %all-gather.8.cloned.1.call-update) | async-done | bytes 2097168 | tf_op jit(solution)/shard_map/all_gather | solution.py:79
  65.1 4.4 fusion.23
  69.6 0.6 fusion.36
  70.2 1.3 collective-permute-start
  71.5 4.1 collective-permute-start.3
  75.6 0.8 collective-permute-done.3
  76.4 2.5 collective-permute-start.4
  78.9 1.0 multiply_cosine_fusion
  79.9 4.4 collective-permute-start.1
  84.4 3.4 collective-permute-start.5
  87.8 1.3 collective-permute-done.5
  89.1 0.1 pad_maximum_fusion
  89.2 4.4 collective-permute-start.2
  93.6 1.4 fusion.14
  95.0 10.2 %collective-permute-done.2 = bf16[1024,256]{0,1:T(8,128)(2,1)S(1)} collective-permute-done((bf16[1024,256]{0,1:T(8,128)(2,1)S(1)}, bf16[1024,256]{0,1:T(8,128)(2,1)S(1)}, u32[]{:S(2)}, u32[]{:S(2)}) %collective-permute-start.2) | collective-permute-done | bytes 524320 | tf_op jit(solution)/shard_map/ppermute | solution.py:16
  105.2 1.1 maximum_maximum_fusion
  106.3 44.8 %all-gather.10.cloned.1.call-done = bf16[4096,512]{1,0:T(8,128)(2,1)} async-done(((bf16[512,512]{1,0:T(8,128)(2,1)}), bf16[4096,512]{1,0:T(8,128)(2,1)}) %all-gather.10.cloned.1.call-update) | async-done | bytes 4194320 | tf_op jit(solution)/shard_map/all_gather | solution.py:78
  151.2 5.9 %fusion.21 = f32[512,512]{0,1:T(8,128)S(1)} fusion(bf16[4096,512]{1,0:T(8,128)(2,1)} %all-gather.10.cloned.1.call-done, bf16[512,4096]{1,0:T(8,128)(2,1)} %param.10, f32[4096]{0:T(1024)S(1)} %copy-done.5, f32[512]{0:T(512)S(1)} %add_rsqrt_fusion.1), kind=kOutput, calls=%fused_computation.27 | convolution fusion | flops 2155872256 | bytes 9455616 | tf_op jit(solution)/shard_map/dot_general | solution.py:82
  157.1 0.9 fusion.42
  158.0 1.4 copy.27
  159.4 1.4 copy.28
  160.8 1.5 subtract_convert_fusion
  162.3 5.3 %fusion.2 = (f32[4,512]{1,0:T(4,128)S(1)}, f32[2560,512,4]{1,0,2:T(8,128)S(1)}) fusion(pred[512,2560]{0,1:T(8,128)(4,1)S(1)} %fusion.14, bf16[512,4,64]{2,0,1:T(8,128)(2,1)S(1)} %get-tuple-element.6, bf16[512,4,64]{2,0,1:T(8,128)(2,1)S(1)} %get-tuple-element.5, bf16[2560,256]{0,1:T(8,128)(2,1)} %maximum_maximum_fusion), kind=kOutput, calls=%fused_computation.4 | convolution fusion | flops 1358952448 | bytes 23470080 | tf_op jit(solution)/shard_map/qhd,kd->hqk/dot_general | solution.py:40
  167.6 4.5 fusion
  172.2 6.1 %divide_convert_fusion = bf16[512,4,128]{0,2,1:T(8,128)(2,1)S(1)} fusion(f32[2560,512,4]{1,0,2:T(8,128)S(1)} %get-tuple-element.14, f32[4,512]{1,0:T(4,128)S(1)} %get-tuple-element.13, pred[512,2560]{0,1:T(8,128)(4,1)S(1)} %fusion.14, bf16[2560,256]{0,1:T(8,128)(2,1)S(1)} %copy-done.3, f32[512,4]{0,1:T(4,128)S(1)} %bitcast.48), kind=kOutput, calls=%fused_computation.29 | convolution fusion | flops 1363673088 | bytes 23478272 | tf_op jit(solution)/shard_map/hqk,kd->qhd/dot_general | solution.py:46
  178.3 38.3 %all-gather.12.cloned.1.call-done = bf16[512,4096]{1,0:T(8,128)(2,1)} async-done(((bf16[512,128]{1,0:T(8,128)(2,1)}), bf16[512,4096]{1,0:T(8,128)(2,1)}) %all-gather.12.cloned.1.call-update) | async-done | bytes 4194320 | tf_op jit(solution)/shard_map/all_gather | solution.py:109
  216.7 5.9 %fusion.9 = bf16[512,4096]{1,0:T(8,128)(2,1)S(1)} fusion(bf16[512,4096]{1,0:T(8,128)(2,1)} %param.10, bf16[512,512]{0,1:T(8,128)(2,1)S(1)} %bitcast.47, bf16[512,4096]{1,0:T(8,128)(2,1)} %all-gather.12.cloned.1.call-done), kind=kOutput, calls=%fused_computation.16 | convolution fusion | flops 2153775104 | bytes 13107200 | tf_op jit(solution)/shard_map/dot_general | solution.py:107
  222.6 2.0 copy-done
  224.6 0.9 fusion.10
  225.5 69.2 %all-gather.18.cloned.1.call-done = bf16[32768,128]{1,0:T(8,128)(2,1)} async-done(((bf16[1024,128]{1,0:T(8,128)(2,1)}), bf16[32768,128]{1,0:T(8,128)(2,1)}) %all-gather.18.cloned.1.call-update) | async-done | bytes 8388624 | tf_op jit(solution)/shard_map/all_gather | solution.py:125
  294.6 11.3 %copy.23 = bf16[1024,32,128]{0,2,1:T(8,128)(2,1)} copy(bf16[1024,32,128]{2,0,1:T(8,128)(2,1)} %bitcast.44) | data formatting | bytes 16777216 | tf_op jit(solution)/shard_map/reshape | solution.py:125
  305.9 67.1 %all-gather.14.cloned.1.call-done = bf16[4096,1024]{1,0:T(8,128)(2,1)} async-done(((bf16[128,1024]{1,0:T(8,128)(2,1)}), bf16[4096,1024]{1,0:T(8,128)(2,1)}) %all-gather.14.cloned.1.call-update) | async-done | bytes 8388624 | tf_op jit(solution)/shard_map/all_gather | solution.py:116
  373.0 10.5 %fusion.19 = f32[512,1024]{1,0:T(8,128)} fusion(bf16[4096,1024]{1,0:T(8,128)(2,1)} %all-gather.14.cloned.1.call-done, bf16[512,4096]{1,0:T(8,128)(2,1)} %copy-done, f32[4096]{0:T(1024)S(1)} %copy-done.6, f32[512]{0:T(512)S(1)} %add_rsqrt_fusion), kind=kOutput, calls=%fused_computation.26 | convolution fusion | flops 4303355904 | bytes 14698496 | tf_op jit(solution)/shard_map/dot_general | solution.py:120
  383.6 67.9 %all-gather.16.cloned.1.call-done = bf16[4096,1024]{1,0:T(8,128)(2,1)} async-done(((bf16[128,1024]{1,0:T(8,128)(2,1)}), bf16[4096,1024]{1,0:T(8,128)(2,1)}) %all-gather.16.cloned.1.call-update) | async-done | bytes 8388624 | tf_op jit(solution)/shard_map/all_gather | solution.py:117
  451.5 11.0 %multiply_convert_fusion = bf16[512,1024]{1,0:T(8,128)(2,1)} fusion(f32[512,1024]{1,0:T(8,128)} %fusion.19, bf16[4096,1024]{1,0:T(8,128)(2,1)} %all-gather.16.cloned.1.call-done, bf16[512,4096]{1,0:T(8,128)(2,1)} %copy-done, f32[4096]{0:T(1024)S(1)} %copy-done.6, f32[512]{0:T(512)S(1)} %add_rsqrt_fusion), kind=kOutput, calls=%fused_computation.23 | convolution fusion | flops 4306501632 | bytes 15747072 | tf_op jit(solution)/shard_map/dot_general | solution.py:121
  462.4 7.3 %fusion.13 = bf16[512,4096]{1,0:T(8,128)(2,1)} fusion(bf16[512,4096]{1,0:T(8,128)(2,1)S(1)} %copy-done.1, bf16[512,1024]{1,0:T(8,128)(2,1)} %multiply_convert_fusion, bf16[1024,4096]{0,1:T(8,128)(2,1)S(1)} %bitcast.45), kind=kOutput, calls=%fused_computation.20 | convolution fusion | flops 4301258752 | bytes 17825792 | tf_op jit(solution)/shard_map/dot_general | solution.py:123
  (31 shorter events, 0.2 us)
Async XLA Ops:
  6.5 58.6 %copy-start.5 = (f32[4096]{0:T(1024)S(1)}, f32[4096]{0:T(1024)}, u32[]{:S(2)}) copy-start(f32[4096]{0:T(1024)} %param.12) | copy-start | bytes 49156
  6.5 58.6 %all-gather.8.cloned.1.call-start = ((), (), s32[]{:S(2)}) async-start(), calls=%async_computation | async-start | bytes 2359296 | tf_op jit(solution)/shard_map/all_gather | solution.py:79
  15.5 135.7 %all-gather.10.cloned.1.call-start = ((), (), s32[]{:S(2)}) async-start(), calls=%async_computation.1 | async-start | bytes 4718592 | tf_op jit(solution)/shard_map/all_gather | solution.py:78
  23.9 192.8 %all-gather.12.cloned.1.call-start = ((), (), s32[]{:S(2)}) async-start(), calls=%async_computation.2 | async-start | bytes 4325376 | tf_op jit(solution)/shard_map/all_gather | solution.py:109
  24.6 270.0 %all-gather.18.cloned.1.call-start = ((), (), s32[]{:S(2)}) async-start(), calls=%async_computation.5 | async-start | bytes 8650752 | tf_op jit(solution)/shard_map/all_gather | solution.py:125
  25.2 347.8 %all-gather.14.cloned.1.call-start = ((), (), s32[]{:S(2)}) async-start(), calls=%async_computation.3 | async-start | bytes 8650752 | tf_op jit(solution)/shard_map/all_gather | solution.py:116
  25.8 425.7 %all-gather.16.cloned.1.call-start = ((), (), s32[]{:S(2)}) async-start(), calls=%async_computation.4 | async-start | bytes 8650752 | tf_op jit(solution)/shard_map/all_gather | solution.py:117
  29.5 42.0 %copy-start.4 = (s32[512]{0:T(512)S(1)}, s32[512]{0:T(512)}, u32[]{:S(2)}) copy-start(s32[512]{0:T(512)} %param.11) | copy-start | bytes 6148
  70.2 9.7 %collective-permute-start = (bf16[512,256]{0,1:T(8,128)(2,1)S(1)}, bf16[512,256]{0,1:T(8,128)(2,1)S(1)}, u32[]{:S(2)}, u32[]{:S(2)}) collective-permute-start(bf16[512,256]{0,1:T(8,128)(2,1)S(1)} %pad_maximum_fusion.1), channel_id=1, source_target_pairs={{0,1},{1,2},{2,3},{3,4},{4,5},{5,6},{6,7},{7,8},{8,9},{9,10},{10,1... | collective-permute-start | bytes 786440 | tf_op jit(solution)/shard_map/ppermute | solution.py:16
  71.5 4.9 %collective-permute-start.3 = (s32[512]{0:T(512)S(1)}, s32[512]{0:T(512)S(1)}, u32[]{:S(2)}, u32[]{:S(2)}) collective-permute-start(s32[512]{0:T(512)S(1)} %broadcast_add_fusion), channel_id=1, source_target_pairs={{0,1},{1,2},{2,3},{3,4},{4,5},{5,6},{6,7},{7,8},{8,9},{9,10},{10,1... | collective-permute-start | bytes 6152 | tf_op jit(solution)/shard_map/ppermute | solution.py:16
  76.4 7.9 %collective-permute-start.4 = (s32[512]{0:T(512)S(1)}, s32[512]{0:T(512)S(1)}, u32[]{:S(2)}, u32[]{:S(2)}) collective-permute-start(s32[512]{0:T(512)S(1)} %collective-permute-done.3), channel_id=1, source_target_pairs={{0,1},{1,2},{2,3},{3,4},{4,5},{5,6},{6,7},{7,8},{8,9},{9,10},{10,1... | collective-permute-start | bytes 6152 | tf_op jit(solution)/shard_map/ppermute | solution.py:16
  79.9 9.2 %collective-permute-start.1 = (bf16[512,256]{0,1:T(8,128)(2,1)S(1)}, bf16[512,256]{0,1:T(8,128)(2,1)S(1)}, u32[]{:S(2)}, u32[]{:S(2)}) collective-permute-start(bf16[512,256]{0,1:T(8,128)(2,1)S(1)} %collective-permute-done), channel_id=1, source_target_pairs={{0,1},{1,2},{2,3},{3,4},{4,5},{5,6},{6,7},{7,8},{8,9},{9,10},{10,1... | collective-permute-start | bytes 786440 | tf_op jit(solution)/shard_map/ppermute | solution.py:16
  84.4 4.8 collective-permute-start.5
  89.2 16.0 %collective-permute-start.2 = (bf16[1024,256]{0,1:T(8,128)(2,1)S(1)}, bf16[1024,256]{0,1:T(8,128)(2,1)S(1)}, u32[]{:S(2)}, u32[]{:S(2)}) collective-permute-start(bf16[1024,256]{0,1:T(8,128)(2,1)S(1)} %pad_maximum_fusion), channel_id=1, source_target_pairs={{0,2},{1,3},{2,4},{3,5},{4,6},{5,7},{6,8},{7,9},{8,10},{9,11},{10,... | collective-permute-start | bytes 1572872 | tf_op jit(solution)/shard_map/ppermute | solution.py:16
  167.6 4.6 copy-start.3
  222.5 2.0 copy-start
  294.6 78.4 %copy-start.6 = (f32[4096]{0:T(1024)S(1)}, f32[4096]{0:T(1024)}, u32[]{:S(2)}) copy-start(f32[4096]{0:T(1024)} %param.13) | copy-start | bytes 49156
  451.5 11.0 %copy-start.1 = (bf16[512,4096]{1,0:T(8,128)(2,1)S(1)}, bf16[512,4096]{1,0:T(8,128)(2,1)}, u32[]{:S(2)}) copy-start(bf16[512,4096]{1,0:T(8,128)(2,1)} %copy-done) | copy-start | bytes 12582916
  451.5 11.0 %copy-start.2 = (bf16[1024,32,128]{0,2,1:T(8,128)(2,1)S(1)}, bf16[1024,32,128]{0,2,1:T(8,128)(2,1)}, u32[]{:S(2)}) copy-start(bf16[1024,32,128]{0,2,1:T(8,128)(2,1)} %copy.23) | copy-start | bytes 25165828
Sparse Core Ops, SparseCore 0:
  15.6 49.3 all-gather.7
  67.2 83.9 all-gather.9
  154.0 62.5 all-gather.11
  219.4 75.2 all-gather.17
  297.3 75.6 all-gather.13
  375.7 75.6 all-gather.15
